TPU v7x, 32 devices: a whole 2x2x4 slice. The times are simulated.
32 devices in a mesh: seq: 8 (over y, x, core), head: 4 (over z).
Axes of the slice: x: 2, y: 2, z: 4, core: 2. Of those that a mesh axis runs over, the one named last changes fastest.
Arguments:
- segment_input: bfloat16 [2, 2048, 3584], P(None, 'seq'), may hold values from -16 to 16
- doc_ids: int32 [2, 2048], replicated, may hold values from 0 to 3, never falling along the last dimension, each value on 1 to 1024 neighbouring positions
- memory: bfloat16 [32, 3584], replicated, may hold values from -16 to 16
- gain: bfloat16 [3584], replicated, may hold values from 0.099609375 to 1.8984375
- w_query: bfloat16 [3584, 4096], P(None, 'head'), may hold values from -4 to 4
- w_key: bfloat16 [3584, 2048], P(None, 'head'), may hold values from -4 to 4
- w_value: bfloat16 [3584, 2048], P(None, 'head'), may hold values from -0.09375 to 0.09375
- w_out: bfloat16 [4096, 3584], P(None, 'head'), may hold values from -0.09375 to 0.09375
- mem_proj: bfloat16 [3584, 3584], P('head'), may hold values from -4 to 4
Outputs:
- hidden: bfloat16 [2, 2048, 3584], P(None, 'seq', 'head')
- new_memory: bfloat16 [32, 3584], replicated
Inputs may be any that keep to these rules, and one draw needn't show every extreme that they name: `doc_ids`: ids never fall along a segment; each document has 1 to 1024 tokens.
All inputs are finite; a program needn't handle non-finite values.
Results may differ from a plain program's by a relative error of at most 0.02.
Values may be sent and summed in bfloat16 or wider, within the bound.
A program may use at most 128 MiB of HBM per device.

v0:
```python
import jax
import jax.numpy as jnp
from jax import lax
from jax.sharding import PartitionSpec as P

HD = 256


def rms_norm(rows, gain):
    values = rows.astype(jnp.float32)
    scaled = values * lax.rsqrt(jnp.mean(values * values, axis=-1, keepdims=True) + 1e-06)
    return (scaled * gain.astype(jnp.float32)).astype(jnp.bfloat16)


def combine(first, second):
    peak = jnp.maximum(first[0], second[0])
    left = jnp.exp(first[0] - peak)
    right = jnp.exp(second[0] - peak)
    return (
        peak,
        first[1] * left + second[1] * right,
        first[2] * left[..., None] + second[2] * right[..., None],
    )


def partial_block(query, keys, values, valid):
    scale = jnp.float32(HD ** (-0.5))
    key_heads = keys.reshape(keys.shape[0], -1, HD)
    value_heads = values.reshape(values.shape[0], -1, HD)
    scores = (
        jnp.einsum("rhgd,khd->hgrk", query, key_heads, preferred_element_type=jnp.float32) * scale
    )
    scores = jnp.where(valid[None, None], scores, -1e30)
    peak = jnp.max(scores, axis=-1)
    weights = jnp.where(valid[None, None], jnp.exp(scores - peak[..., None]), 0.0)
    total = jnp.sum(weights, axis=-1)
    mixed = jnp.einsum(
        "hgrk,khd->hgrd",
        weights.astype(jnp.bfloat16),
        value_heads,
        preferred_element_type=jnp.float32,
    )
    return (peak, total, mixed)


def finish(state):
    mixed = state[2] / state[1][..., None]
    return mixed.transpose(2, 0, 1, 3).reshape(mixed.shape[2], -1).astype(jnp.bfloat16)


def per_device(segment_input, doc_ids, memory, gain, w_query, w_key, w_value, w_out, mem_proj):
    tok_rows = segment_input.shape[1]
    columns = w_out.shape[1]
    kv_local = w_key.shape[1] // HD
    col_start = lax.axis_index("head") * columns
    row_start = lax.axis_index("seq") * tok_rows
    my_pos = row_start + jnp.arange(tok_rows, dtype=jnp.int32)
    mem = memory
    outputs = []
    for seg in range(segment_input.shape[0]):
        tokens = segment_input[seg]
        docs = doc_ids[seg]
        my_docs = lax.dynamic_slice_in_dim(docs, row_start, tok_rows, 0)
        normed_x = rms_norm(tokens, gain)
        normed_m = rms_norm(mem, gain)
        query = (
            jnp.dot(normed_x, w_query, preferred_element_type=jnp.float32)
            .astype(jnp.bfloat16)
            .reshape(tok_rows, kv_local, 2, HD)
        )
        keys = jnp.dot(normed_x, w_key, preferred_element_type=jnp.float32).astype(jnp.bfloat16)
        values = jnp.dot(normed_x, w_value, preferred_element_type=jnp.float32).astype(jnp.bfloat16)
        mem_query = (
            jnp.dot(normed_m, w_query, preferred_element_type=jnp.float32)
            .astype(jnp.bfloat16)
            .reshape(mem.shape[0], kv_local, 2, HD)
        )
        mem_keys = jnp.dot(normed_m, w_key, preferred_element_type=jnp.float32).astype(jnp.bfloat16)
        mem_values = jnp.dot(normed_m, w_value, preferred_element_type=jnp.float32).astype(
            jnp.bfloat16
        )
        open_tok = jnp.ones((tok_rows, mem.shape[0]), dtype=bool)
        open_mem = jnp.ones((mem.shape[0], mem.shape[0]), dtype=bool)
        tok_init = partial_block(query, mem_keys, mem_values, open_tok)
        mem_init = partial_block(mem_query, mem_keys, mem_values, open_mem)
        both_pieces = (
            lax.all_gather(keys, "seq", axis=0, tiled=True),
            lax.all_gather(values, "seq", axis=0, tiled=True),
        )
        open_keys = jnp.ones((mem.shape[0], both_pieces[0].shape[0]), dtype=bool)
        written = combine(
            mem_init, partial_block(mem_query, both_pieces[0], both_pieces[1], open_keys)
        )
        key_piece, value_piece = both_pieces
        key_pos = jnp.arange(key_piece.shape[0], dtype=jnp.int32)
        valid = (key_pos[None, :] <= my_pos[:, None]) & (docs[None, :] == my_docs[:, None])
        tok_state = combine(tok_init, partial_block(query, key_piece, value_piece, valid))
        attn_tok = finish(tok_state)
        attn_mem = finish(written)
        out_tok = jnp.dot(
            lax.all_gather(attn_tok, "head", axis=1, tiled=True),
            w_out,
            preferred_element_type=jnp.float32,
        )
        out_mem = jnp.dot(
            lax.all_gather(attn_mem, "head", axis=1, tiled=True),
            w_out,
            preferred_element_type=jnp.float32,
        )
        token_cols = lax.dynamic_slice_in_dim(tokens, col_start, columns, 1).astype(jnp.float32)
        outputs.append((token_cols + out_tok).astype(jnp.bfloat16))
        mem_cols = lax.dynamic_slice_in_dim(mem, col_start, columns, 1).astype(jnp.float32)
        mem_out = (mem_cols + out_mem).astype(jnp.bfloat16)
        partial_mem = jnp.dot(mem_out, mem_proj, preferred_element_type=jnp.float32)
        mem = lax.psum(partial_mem.astype(jnp.bfloat16), "head")
    return (jnp.stack(outputs, axis=0), mem)


def solution(mesh):
    return jax.shard_map(
        per_device,
        mesh=mesh,
        in_specs=(
            P(None, "seq", None),
            P(),
            P(),
            P(),
            P(None, "head"),
            P(None, "head"),
            P(None, "head"),
            P(None, "head"),
            P("head", None),
        ),
        out_specs=(P(None, "seq", "head"), P()),
        check_vma=False,
    )
```

profile of v0, /device:TPU:0, one launch (start us, length us, event | category | flops | bytes accessed | tf_op | source)
XLA Modules:
  0.0 315.8 jit_solution(6064854172104741150)
XLA Ops:
  11.1 3.9 %convolution_convert_fusion.7 = bf16[256,512]{1,0:T(8,128)(2,1)} fusion(bf16[3584,512]{1,0:T(8,128)(2,1)} %param.14, f32[3584]{0:T(1024)S(1)} %convert_element_type.159, f32[256]{0:T(256)S(1)} %add_rsqrt_fusion.1, bf16[2,256,3584]{2,1,0:T(8,128)(2,1)S(1)} %copy-done), kind=kOutput, calls=%fused_computation.64 | convolution fusion | flops 943325184 | bytes 5784576 | tf_op jit(solution)/shard_map/dot_general | solution.py:71
  15.1 4.5 %convolution_convert_fusion.6 = bf16[256,512]{1,0:T(8,128)(2,1)} fusion(bf16[3584,512]{1,0:T(8,128)(2,1)} %param.15, f32[3584]{0:T(1024)S(1)} %convert_element_type.159, f32[256]{0:T(256)S(1)} %add_rsqrt_fusion.1, bf16[2,256,3584]{2,1,0:T(8,128)(2,1)} %param.9), kind=kOutput, calls=%fused_computation.63 | convolution fusion | flops 943325184 | bytes 5782528 | tf_op jit(solution)/shard_map/dot_general | solution.py:72
  19.7 4.5 %convolution_convert_fusion.5 = bf16[256,512]{1,0:T(8,128)(2,1)} fusion(bf16[3584,512]{1,0:T(8,128)(2,1)} %param.14, f32[256]{0:T(256)S(1)} %add_rsqrt_fusion, f32[3584]{0:T(1024)S(1)} %convert_element_type.159, bf16[2,256,3584]{2,1,0:T(8,128)(2,1)} %param.9), kind=kOutput, calls=%fused_computation.62 | convolution fusion | flops 943325184 | bytes 5782528 | tf_op jit(solution)/shard_map/dot_general | solution.py:71
  24.2 4.7 %convolution_convert_fusion.4 = bf16[256,512]{1,0:T(8,128)(2,1)} fusion(bf16[3584,512]{1,0:T(8,128)(2,1)} %param.15, f32[256]{0:T(256)S(1)} %add_rsqrt_fusion, f32[3584]{0:T(1024)S(1)} %convert_element_type.159, bf16[2,256,3584]{2,1,0:T(8,128)(2,1)} %param.9), kind=kOutput, calls=%fused_computation.61 | convolution fusion | flops 943325184 | bytes 5782528 | tf_op jit(solution)/shard_map/dot_general | solution.py:72
  33.2 4.8 %convolution_convert_fusion.9 = bf16[32,1024]{1,0:T(8,128)(2,1)S(1)} fusion(bf16[3584,1024]{1,0:T(8,128)(2,1)} %param.13, bf16[32,3584]{1,0:T(8,128)(2,1)S(1)} %copy-done.7, f32[3584]{0:T(1024)S(1)} %convert_element_type.159, f32[32]{0:T(128)S(1)} %add_rsqrt_fusion.3), kind=kOutput, calls=%fused_computation.86 | convolution fusion | flops 235372544 | bytes 7649408 | tf_op jit(solution)/shard_map/dot_general | solution.py:74
  52.4 23.1 %all-gather.9.cloned.1.call-done = bf16[2048,512]{1,0:T(8,128)(2,1)} async-done(((bf16[256,512]{1,0:T(8,128)(2,1)}), bf16[2048,512]{1,0:T(8,128)(2,1)}) %all-gather.9.cloned.1.call-update) | async-done | bytes 2097168 | tf_op jit(solution)/shard_map/all_gather | solution.py:88
  75.4 4.0 %reshape.313 = bf16[2048,2,256]{2,1,0:T(2,128)(2,1)} reshape(bf16[2048,512]{1,0:T(8,128)(2,1)} %all-gather.9.cloned.1.call-done) | data formatting | bytes 4194304 | tf_op jit(solution)/shard_map/reshape | solution.py:29
  79.4 4.7 %copy.73 = bf16[2048,2,256,1]{0,2,3,1:T(8,128)(2,1)S(1)} copy(bf16[2048,2,256,1]{2,1,0,3:T(2,128)(2,1)} %bitcast.248) | data formatting | bytes 4194304 | tf_op jit(solution)/shard_map/reshape | solution.py:29
  85.6 14.1 %all_gather.27 = bf16[32,4096]{1,0:T(8,128)(2,1)S(1)} all-gather(bf16[32,1024]{1,0:T(8,128)(2,1)S(1)} %convert_element_type.181), channel_id=1, replica_groups=mesh['seq'=8,'head'=4] {'head'}, dimensions={1}, use_global_device_ids=true | all-gather | bytes 327680 | tf_op jit(solution)/shard_map/all_gather | solution.py:106
  99.7 3.5 %fusion = (f32[2,2,256]{2,1,0:T(2,128)S(1)}, f32[2,2048,256,2]{2,1,3,0:T(8,128)S(1)}) fusion(pred[256,2048]{0,1:T(8,128)(4,1)} %get-tuple-element.20, bf16[256,2,2,256]{3,2,1,0:T(2,128)(2,1)} %copy-done.12, bf16[2048,2,256,1]{2,1,0,3:T(2,128)(2,1)} %bitcast.247), kind=kOutput, calls=%fused_computation.4 | convolution fusion | flops 1080032256 | bytes 11538432 | tf_op jit(solution)/shard_map/rhgd,khd->hgrk/dot_general | solution.py:31
  106.5 8.0 %convolution_convert_fusion.1 = bf16[32,3584]{1,0:T(8,128)(2,1)} fusion(bf16[896,3584]{1,0:T(8,128)(2,1)} %param.17, bf16[32,4096]{1,0:T(8,128)(2,1)S(1)} %all_gather.27, bf16[4096,896]{1,0:T(8,128)(2,1)} %param.16, bf16[32,3584]{1,0:T(8,128)(2,1)S(1)} %copy-done.7, s32[]{:T(128)S(6)} %select_n.38), kind=kOutput, calls=%fused_computation.15 | convolution fusion | flops 440602624 | bytes 14311428 | tf_op jit(solution)/shard_map/dot_general | solution.py:114
  114.5 7.0 %fusion.43 = f32[256,2,2,256]{0,3,2,1:T(8,128)} fusion(bf16[2048,2,256,1]{0,2,3,1:T(8,128)(2,1)S(1)} %copy.73, f32[2,2048,256,2]{2,1,3,0:T(8,128)} %copy-done.4, f32[2,2,256]{2,1,0:T(2,128)S(1)} %get-tuple-element.30, pred[256,2048]{0,1:T(8,128)(4,1)S(1)} %copy-done.10, f32[256,2,2]{0,2,1:T(2,128)S(1)} %get-tuple-element.9), kind=kOutput, calls=%fused_computation.50 | convolution fusion | flops 1084489728 | bytes 12066816 | tf_op jit(solution)/shard_map/hgrk,khd->hgrd/dot_general | solution.py:37
  134.7 4.0 %reshape.319 = bf16[2048,2,256]{2,1,0:T(2,128)(2,1)} reshape(bf16[2048,512]{1,0:T(8,128)(2,1)} %all-gather.15.cloned.1.call-done) | data formatting | bytes 4194304 | tf_op jit(solution)/shard_map/reshape | solution.py:29
  138.7 4.7 %copy.83 = bf16[2048,2,256,1]{0,2,3,1:T(8,128)(2,1)S(1)} copy(bf16[2048,2,256,1]{2,1,0,3:T(2,128)(2,1)} %bitcast.249) | data formatting | bytes 4194304 | tf_op jit(solution)/shard_map/reshape | solution.py:29
  143.4 29.2 %all-reduce.3.cloned.1.call-done = bf16[32,3584]{1,0:T(8,128)(2,1)} async-done(((bf16[32,3584]{1,0:T(8,128)(2,1)}), bf16[32,3584]{1,0:T(8,128)(2,1)}) %all-reduce.3.cloned.1.call-update) | async-done | bytes 229392 | tf_op jit(solution)/shard_map/psum | solution.py:115
  180.1 5.0 %fusion.40 = f32[256,2,2,256]{0,3,2,1:T(8,128)S(1)} fusion(bf16[2048,2,256,1]{0,2,3,1:T(8,128)(2,1)S(1)} %copy.83, f32[2,2048,256,2]{2,1,3,0:T(8,128)} %copy-done.3, f32[2,2,256]{2,1,0:T(2,128)S(1)} %get-tuple-element.22, pred[256,2048]{0,1:T(8,128)(4,1)S(1)} %copy-done.9, f32[256,2,2]{0,2,1:T(2,128)S(1)} %get-tuple-element.12), kind=kOutput, calls=%fused_computation.49 | convolution fusion | flops 1084489728 | bytes 12066816 | tf_op jit(solution)/shard_map/hgrk,khd->hgrd/dot_general | solution.py:37
  186.3 4.1 %fusion.158 = (bf16[1,256,3584]{2,1,0:T(8,128)(2,1)}, bf16[1,256,3584]{2,1,0:T(8,128)(2,1)}) fusion(bf16[2,256,3584]{2,1,0:T(8,128)(2,1)} %param.9), kind=kLoop, calls=%fused_computation.195 | loop fusion | bytes 7340032 | tf_op jit(solution)/shard_map/slice | solution.py:61
  190.4 4.5 %convolution_convert_fusion.8 = bf16[32,1024]{1,0:T(8,128)(2,1)S(1)} fusion(bf16[3584,1024]{1,0:T(8,128)(2,1)} %param.13, bf16[32,3584]{1,0:T(8,128)(2,1)S(1)} %copy-done.8, f32[32]{0:T(128)S(1)} %add_rsqrt_fusion.2, f32[3584]{0:T(1024)S(1)} %convert_element_type.159), kind=kOutput, calls=%fused_computation.85 | convolution fusion | flops 235372544 | bytes 7649408 | tf_op jit(solution)/shard_map/dot_general | solution.py:74
  199.1 16.7 %all_gather.31 = bf16[32,4096]{1,0:T(8,128)(2,1)S(1)} all-gather(bf16[32,1024]{1,0:T(8,128)(2,1)S(1)} %convert_element_type.204), channel_id=1, replica_groups=mesh['seq'=8,'head'=4] {'head'}, dimensions={1}, use_global_device_ids=true | all-gather | bytes 327680 | tf_op jit(solution)/shard_map/all_gather | solution.py:106
  215.8 8.0 %convolution_convert_fusion = bf16[32,3584]{1,0:T(8,128)(2,1)} fusion(bf16[896,3584]{1,0:T(8,128)(2,1)} %param.17, bf16[32,4096]{1,0:T(8,128)(2,1)S(1)} %all_gather.31, bf16[4096,896]{1,0:T(8,128)(2,1)} %param.16, bf16[32,3584]{1,0:T(8,128)(2,1)S(1)} %copy-done.8, s32[]{:T(128)S(6)} %select_n.38), kind=kOutput, calls=%fused_computation.14 | convolution fusion | flops 440602624 | bytes 14311428 | tf_op jit(solution)/shard_map/dot_general | solution.py:114
  223.8 6.1 %fusion.51 = bf16[1,256,896]{2,1,0:T(8,128)(2,1)S(1)} fusion(bf16[256,4096]{0,1:T(8,128)(2,1)} %all-gather.11.cloned.1.call-done, bf16[4096,896]{1,0:T(8,128)(2,1)} %param.16, bf16[1,256,3584]{2,1,0:T(8,128)(2,1)} %get-tuple-element.16, s32[]{:T(128)S(6)} %select_n.38), kind=kOutput, calls=%fused_computation.60 | convolution fusion | flops 1879736320 | bytes 10354692 | tf_op jit(solution)/shard_map/dot_general | solution.py:100
  230.0 40.4 %all-gather.17.cloned.1.call-done = bf16[256,4096]{0,1:T(8,128)(2,1)} async-done(((bf16[256,1024]{0,1:T(8,128)(2,1)}), bf16[256,4096]{0,1:T(8,128)(2,1)}) %all-gather.17.cloned.1.call-update) | async-done | bytes 2097168 | tf_op jit(solution)/shard_map/all_gather | solution.py:101
  270.4 6.2 %fusion.50 = bf16[1,256,896]{2,1,0:T(8,128)(2,1)S(1)} fusion(bf16[256,4096]{0,1:T(8,128)(2,1)} %all-gather.17.cloned.1.call-done, bf16[4096,896]{1,0:T(8,128)(2,1)} %param.16, bf16[1,256,3584]{2,1,0:T(8,128)(2,1)} %get-tuple-element.17, s32[]{:T(128)S(6)} %select_n.38), kind=kOutput, calls=%fused_computation.59 | convolution fusion | flops 1879736320 | bytes 10354692 | tf_op jit(solution)/shard_map/dot_general | solution.py:100
  277.6 29.7 %all-reduce.5.cloned.1.call-done = bf16[32,3584]{1,0:T(8,128)(2,1)} async-done(((bf16[32,3584]{1,0:T(8,128)(2,1)}), bf16[32,3584]{1,0:T(8,128)(2,1)}) %all-reduce.5.cloned.1.call-update) | async-done | bytes 229392 | tf_op jit(solution)/shard_map/psum | solution.py:115
  (130 shorter events, 55.6 us)
Async XLA Ops:
  7.2 41.2 %all-gather.7.cloned.1.call-start = ((), (), s32[]{:S(2)}) async-start(), calls=%async_computation | async-start | bytes 2359296 | tf_op jit(solution)/shard_map/all_gather | solution.py:87
  15.1 60.4 %all-gather.9.cloned.1.call-start = ((), (), s32[]{:S(2)}) async-start(), calls=%async_computation.1 | async-start | bytes 2359296 | tf_op jit(solution)/shard_map/all_gather | solution.py:88
  19.6 104.8 %all-gather.13.cloned.1.call-start = ((), (), s32[]{:S(2)}) async-start(), calls=%async_computation.4 | async-start | bytes 2359296 | tf_op jit(solution)/shard_map/all_gather | solution.py:87
  24.2 5.0 %copy-start.7 = (bf16[32,3584]{1,0:T(8,128)(2,1)S(1)}, bf16[32,3584]{1,0:T(8,128)(2,1)}, u32[]{:S(2)}) copy-start(bf16[32,3584]{1,0:T(8,128)(2,1)} %param.11) | copy-start | bytes 688132
  24.2 110.5 %all-gather.15.cloned.1.call-start = ((), (), s32[]{:S(2)}) async-start(), calls=%async_computation.5 | async-start | bytes 2359296 | tf_op jit(solution)/shard_map/all_gather | solution.py:88
  29.0 143.7 %all-reduce.3.cloned.1.call-start = ((), (), s32[]{:S(2)}) async-start(), calls=%async_computation.3 | async-start | bytes 458752 | tf_op jit(solution)/shard_map/psum | solution.py:115
  29.4 8.6 %slice-start = ((s8[7340032]{0:T(1024)(128)(4,1)}), s8[4194304]{0:T(1024)(128)(4,1)S(1)}, s32[]{:S(2)}) async-start(s8[7340032]{0:T(1024)(128)(4,1)} %bitcast.242), calls=%async_computation.8 | async-start | bytes 8388608
  32.4 5.6 %slice-start.1 = ((s8[7340032]{0:T(1024)(128)(4,1)}), s8[3145728]{0:T(1024)(128)(4,1)S(1)}, s32[]{:S(2)}) async-start(s8[7340032]{0:T(1024)(128)(4,1)} %bitcast.242), calls=%async_computation.9 | async-start | bytes 6291456
  33.2 5.0 %copy-start.1 = (bf16[2,256,3584]{2,1,0:T(8,128)(2,1)S(1)}, bf16[2,256,3584]{2,1,0:T(8,128)(2,1)}, u32[]{:S(2)}) copy-start(bf16[2,256,3584]{2,1,0:T(8,128)(2,1)} %param.9) | copy-start | bytes 11010052
  43.0 7.9 %copy-start.12 = (bf16[256,2,2,256]{3,2,1,0:T(2,128)(2,1)}, bf16[256,2,2,256]{3,2,1,0:T(2,128)(2,1)S(1)}, u32[]{:S(2)}) copy-start(bf16[256,2,2,256]{3,2,1,0:T(2,128)(2,1)S(1)} %reshape.310) | copy-start | bytes 1572868
  43.2 5.1 %copy-start.17 = (f32[2,2,32]{2,1,0:T(2,128)}, f32[2,2,32]{2,1,0:T(2,128)S(1)}, u32[]{:S(2)}) copy-start(f32[2,2,32]{2,1,0:T(2,128)S(1)} %get-tuple-element.26) | copy-start | bytes 1540
  43.5 4.8 %copy-start.13 = (f32[2,2,256,32]{2,3,1,0:T(8,128)}, f32[2,2,256,32]{2,3,1,0:T(8,128)S(1)}, u32[]{:S(2)}) copy-start(f32[2,2,256,32]{2,3,1,0:T(8,128)S(1)} %get-tuple-element.33) | copy-start | bytes 393220
  43.5 4.8 %copy-start.15 = (f32[2,2,256]{2,1,0:T(2,128)}, f32[2,2,256]{2,1,0:T(2,128)S(1)}, u32[]{:S(2)}) copy-start(f32[2,2,256]{2,1,0:T(2,128)S(1)} %get-tuple-element.32) | copy-start | bytes 12292
  50.9 28.5 %copy-start.6 = (bf16[2048,2,256]{2,1,0:T(2,128)(2,1)}, bf16[2048,2,256]{2,1,0:T(2,128)(2,1)S(1)}, u32[]{:S(2)}) copy-start(bf16[2048,2,256]{2,1,0:T(2,128)(2,1)S(1)} %reshape.312) | copy-start | bytes 6291460
  52.4 31.8 %copy-start.19 = (f32[2,2,32]{2,1,0:T(2,128)S(1)}, f32[2,2,32]{2,1,0:T(2,128)}, u32[]{:S(2)}) copy-start(f32[2,2,32]{2,1,0:T(2,128)} %get-tuple-element.24) | copy-start | bytes 1540
  79.4 5.1 %copy-start.18 = (f32[2,2,32]{2,1,0:T(2,128)S(1)}, f32[2,2,32]{2,1,0:T(2,128)}, u32[]{:S(2)}) copy-start(f32[2,2,32]{2,1,0:T(2,128)} %copy-done.17) | copy-start | bytes 1540
  79.4 5.1 %copy-start.22 = (f32[2,2,32]{2,1,0:T(2,128)S(1)}, f32[2,2,32]{2,1,0:T(2,128)}, u32[]{:S(2)}) copy-start(f32[2,2,32]{2,1,0:T(2,128)} %fusion.96) | copy-start | bytes 1540
  114.5 7.1 %copy-start.14 = (f32[2,2,256,32]{2,3,1,0:T(8,128)S(1)}, f32[2,2,256,32]{2,3,1,0:T(8,128)}, u32[]{:S(2)}) copy-start(f32[2,2,256,32]{2,3,1,0:T(8,128)} %copy-done.13) | copy-start | bytes 393220
  121.5 102.3 %all-gather.11.cloned.1.call-start = ((), (), s32[]{:S(2)}) async-start(), calls=%async_computation.2 | async-start | bytes 2621440 | tf_op jit(solution)/shard_map/all_gather | solution.py:101
  121.6 5.5 %copy-start.9 = (pred[256,2048]{0,1:T(8,128)(4,1)S(1)}, pred[256,2048]{0,1:T(8,128)(4,1)}, u32[]{:S(2)}) copy-start(pred[256,2048]{0,1:T(8,128)(4,1)} %get-tuple-element.21) | copy-start | bytes 1572868
  121.6 5.5 %copy-start.11 = (bf16[256,2,2,256]{3,2,1,0:T(2,128)(2,1)S(1)}, bf16[256,2,2,256]{3,2,1,0:T(2,128)(2,1)}, u32[]{:S(2)}) copy-start(bf16[256,2,2,256]{3,2,1,0:T(2,128)(2,1)} %reshape.316) | copy-start | bytes 1572868
  124.1 146.3 %all-gather.17.cloned.1.call-start = ((), (), s32[]{:S(2)}) async-start(), calls=%async_computation.6 | async-start | bytes 2621440 | tf_op jit(solution)/shard_map/all_gather | solution.py:101
  172.7 4.2 %copy-start.8 = (bf16[32,3584]{1,0:T(8,128)(2,1)S(1)}, bf16[32,3584]{1,0:T(8,128)(2,1)}, u32[]{:S(2)}) copy-start(bf16[32,3584]{1,0:T(8,128)(2,1)} %all-reduce.3.cloned.1.call-done) | copy-start | bytes 688132
  186.2 121.1 %all-reduce.5.cloned.1.call-start = ((), (), s32[]{:S(2)}) async-start(), calls=%async_computation.7 | async-start | bytes 458752 | tf_op jit(solution)/shard_map/psum | solution.py:115
  (9 other events, 27.4 us)
Sparse Core Ops, SparseCore 0:
  15.2 30.4 all-gather.6
  47.6 27.7 all-gather.8
  77.3 27.7 all-gather.12
  106.9 27.7 all-gather.14
  137.4 35.1 all-reduce.2
  174.1 49.5 all-gather.10
  225.9 44.4 all-gather.16
  273.3 33.9 all-reduce.4
where the time goes:
time: 317 us; the launch traced here: 316 us
  waiting for transfers between devices  123 us (39%)
  matrix products  96.5 us (30%)
  local copies, waits for them, and re-layouts  34.9 us (11%)
  blocking collectives  30.8 us (10%)
  other arithmetic  14.7 us (5%)
  between operations  14.7 us (5%)
    psum x2, waiting for transfers between devices, per_device(): mem = lax.psum(partial_mem.astype(jnp.bfloat16), 'head')  59 us
    all_gather x2, waiting for transfers between devices, per_device(): lax.all_gather(attn_tok, 'head', axis=1, tiled=True)  40.4 us
    all_gather x2, blocking collectives, per_device(): lax.all_gather(attn_mem, 'head', axis=1, tiled=True)  30.8 us
    all_gather x2, waiting for transfers between devices, per_device(): lax.all_gather(values, 'seq', axis=0, tiled=True)  23.8 us
    dot_general x8, matrix products, partial_block(): jnp.einsum('hgrk,khd->hgrd', weights.astype(jnp.bfloat16), value_heads, p...  17.6 us
    reshape x6, local copies, waits for them, and re-layouts, partial_block(): value_heads = values.reshape(values.shape[0], -1, HD)  17.5 us
    dot_general x2, matrix products, per_device(): partial_mem = jnp.dot(mem_out, mem_proj, preferred_element_type=jnp.float32)  16 us
    dot_general x2, matrix products, per_device(): jnp.dot(lax.all_gather(attn_tok, 'head', axis=1, tiled=True), w_out, pref...  12.3 us
  transfers between devices with their start and end apart: 8, of which 5 were waited for; matrix products, arithmetic and copies ran while one was open for 42% of the time, Pallas kernels for 0%

commit v1 on v0

--- a/solution.py
+++ b/solution.py
@@ -112,7 +112,7 @@
         mem_cols = lax.dynamic_slice_in_dim(mem, col_start, columns, 1).astype(jnp.float32)
         mem_out = (mem_cols + out_mem).astype(jnp.bfloat16)
         partial_mem = jnp.dot(mem_out, mem_proj, preferred_element_type=jnp.float32)
-        mem = lax.psum(partial_mem.astype(jnp.bfloat16), "head")
+        mem = jnp.sum(lax.all_gather(partial_mem.astype(jnp.bfloat16), "head"), axis=0)
     return (jnp.stack(outputs, axis=0), mem)
 
 

time: 317 us -> 263 us (0.83)
  waiting for transfers between devices: 123 us -> 41.1 us
  blocking collectives: 30.8 us -> 73.6 us
  matrix products: 96.5 us -> 86.5 us
  local copies, waits for them, and re-layouts: 34.9 us -> 30 us
    psum x2 -> x0, waiting for transfers between devices: 59 us -> none  [per_device(): mem = lax.psum(partial_mem.astype(jnp.bfloat16), 'head')]
    all_gather x0 -> x2, blocking collectives: none -> 43.4 us  [per_device(): lax.all_gather(partial_mem.astype(jnp.bfloat16), 'head')]
    all_gather x2, waiting for transfers between devices: 40.4 us -> 19.7 us  [per_device(): lax.all_gather(attn_tok, 'head', axis=1, tiled=True)]
    dot_general x8, matrix products: 17.6 us -> 8.93 us  [partial_block(): jnp.einsum('hgrk,khd->hgrd', weights.astype(jnp.bfloat16), value_heads, p...]
    unnamed x51 -> x62, local copies, waits for them, and re-layouts: 6.22 us -> 1.29 us
  transfers between devices with their start and end apart: 8 -> 6, of which waited for: 5 -> 2; matrix products, arithmetic and copies ran while one was open for 42% -> 44% of each run, Pallas kernels for 0% -> 0%
where the time goes in v1:
time: 263 us; the launch traced here: 262 us
  matrix products  86.5 us (33%)
  blocking collectives  73.6 us (28%)
  waiting for transfers between devices  41.1 us (16%)
  local copies, waits for them, and re-layouts  30 us (11%)
  other arithmetic  15.3 us (6%)
  between operations  14.7 us (6%)
    all_gather x2, blocking collectives, per_device(): lax.all_gather(partial_mem.astype(jnp.bfloat16), 'head')  43.4 us
    all_gather x2, blocking collectives, per_device(): lax.all_gather(attn_mem, 'head', axis=1, tiled=True)  30.2 us
    all_gather x2, waiting for transfers between devices, per_device(): lax.all_gather(values, 'seq', axis=0, tiled=True)  21.2 us
    all_gather x2, waiting for transfers between devices, per_device(): lax.all_gather(attn_tok, 'head', axis=1, tiled=True)  19.7 us
    reshape x6, local copies, waits for them, and re-layouts, partial_block(): value_heads = values.reshape(values.shape[0], -1, HD)  18.2 us
    dot_general x2, matrix products, per_device(): partial_mem = jnp.dot(mem_out, mem_proj, preferred_element_type=jnp.float32)  15.4 us
    dot_general x2, matrix products, per_device(): jnp.dot(lax.all_gather(attn_tok, 'head', axis=1, tiled=True), w_out, pref...  12.4 us
    dot_general x8, matrix products, partial_block(): jnp.einsum('rhgd,khd->hgrk', query, key_heads, preferred_element_type=jnp...  11.2 us
  transfers between devices with their start and end apart: 6, of which 2 were waited for; matrix products, arithmetic and copies ran while one was open for 44% of the time, Pallas kernels for 0%

profile of v1, /device:TPU:0, one launch (start us, length us, event | category | flops | bytes accessed | tf_op | source)
XLA Modules:
  0.0 261.8 jit_solution(6723832080244002121)
XLA Ops:
  8.1 3.0 %fusion.12 = (f32[256]{0:T(256)S(1)}, f32[256]{0:T(256)S(1)}) fusion(bf16[2,256,3584]{2,1,0:T(8,128)(2,1)} %param.9), kind=kLoop, calls=%fused_computation.20 | loop fusion | flops 5504512 | bytes 3672064 | tf_op jit(solution)/shard_map/reduce_sum | solution.py:11
  11.1 3.9 %convolution_convert_fusion.7 = bf16[256,512]{1,0:T(8,128)(2,1)} fusion(bf16[3584,512]{1,0:T(8,128)(2,1)} %param.14, f32[3584]{0:T(1024)S(1)} %convert_element_type.163, f32[256]{0:T(256)S(1)} %add_rsqrt_fusion.1, bf16[2,256,3584]{2,1,0:T(8,128)(2,1)S(1)} %copy-done), kind=kOutput, calls=%fused_computation.64 | convolution fusion | flops 943325184 | bytes 5784576 | tf_op jit(solution)/shard_map/dot_general | solution.py:71
  15.1 4.5 %convolution_convert_fusion.6 = bf16[256,512]{1,0:T(8,128)(2,1)} fusion(bf16[3584,512]{1,0:T(8,128)(2,1)} %param.15, f32[3584]{0:T(1024)S(1)} %convert_element_type.163, f32[256]{0:T(256)S(1)} %add_rsqrt_fusion.1, bf16[2,256,3584]{2,1,0:T(8,128)(2,1)} %param.9), kind=kOutput, calls=%fused_computation.63 | convolution fusion | flops 943325184 | bytes 5782528 | tf_op jit(solution)/shard_map/dot_general | solution.py:72
  19.7 4.5 %convolution_convert_fusion.4 = bf16[256,512]{1,0:T(8,128)(2,1)} fusion(bf16[3584,512]{1,0:T(8,128)(2,1)} %param.15, f32[256]{0:T(256)S(1)} %add_rsqrt_fusion, f32[3584]{0:T(1024)S(1)} %convert_element_type.163, bf16[2,256,3584]{2,1,0:T(8,128)(2,1)} %param.9), kind=kOutput, calls=%fused_computation.61 | convolution fusion | flops 943325184 | bytes 5782528 | tf_op jit(solution)/shard_map/dot_general | solution.py:72
  24.2 4.7 %convolution_convert_fusion.5 = bf16[256,512]{1,0:T(8,128)(2,1)} fusion(bf16[3584,512]{1,0:T(8,128)(2,1)} %param.14, f32[256]{0:T(256)S(1)} %add_rsqrt_fusion, f32[3584]{0:T(1024)S(1)} %convert_element_type.163, bf16[2,256,3584]{2,1,0:T(8,128)(2,1)} %param.9), kind=kOutput, calls=%fused_computation.62 | convolution fusion | flops 943325184 | bytes 5782528 | tf_op jit(solution)/shard_map/dot_general | solution.py:71
  33.2 4.8 %convolution_convert_fusion.9 = bf16[32,1024]{1,0:T(8,128)(2,1)S(1)} fusion(bf16[3584,1024]{1,0:T(8,128)(2,1)} %param.13, bf16[32,3584]{1,0:T(8,128)(2,1)S(1)} %copy-done.5, f32[3584]{0:T(1024)S(1)} %convert_element_type.163, f32[32]{0:T(128)S(1)} %add_rsqrt_fusion.3), kind=kOutput, calls=%fused_computation.86 | convolution fusion | flops 235372544 | bytes 7649408 | tf_op jit(solution)/shard_map/dot_general | solution.py:74
  54.2 21.2 %all-gather.11.cloned.1.call-done = bf16[2048,512]{1,0:T(8,128)(2,1)} async-done(((bf16[256,512]{1,0:T(8,128)(2,1)}), bf16[2048,512]{1,0:T(8,128)(2,1)}) %all-gather.11.cloned.1.call-update) | async-done | bytes 2097168 | tf_op jit(solution)/shard_map/all_gather | solution.py:88
  75.4 4.0 %reshape.313 = bf16[2048,2,256]{2,1,0:T(2,128)(2,1)} reshape(bf16[2048,512]{1,0:T(8,128)(2,1)} %all-gather.11.cloned.1.call-done) | data formatting | bytes 4194304 | tf_op jit(solution)/shard_map/reshape | solution.py:29
  79.4 4.7 %copy.73 = bf16[2048,2,256,1]{0,2,3,1:T(8,128)(2,1)S(1)} copy(bf16[2048,2,256,1]{2,1,0,3:T(2,128)(2,1)} %bitcast.250) | data formatting | bytes 4194304 | tf_op jit(solution)/shard_map/reshape | solution.py:29
  85.6 13.9 %all_gather.39 = bf16[32,4096]{1,0:T(8,128)(2,1)S(1)} all-gather(bf16[32,1024]{1,0:T(8,128)(2,1)S(1)} %convert_element_type.185), channel_id=1, replica_groups=mesh['seq'=8,'head'=4] {'head'}, dimensions={1}, use_global_device_ids=true | all-gather | bytes 327680 | tf_op jit(solution)/shard_map/all_gather | solution.py:106
  99.5 8.1 %convolution_convert_fusion.1 = bf16[32,3584]{1,0:T(8,128)(2,1)} fusion(bf16[896,3584]{1,0:T(8,128)(2,1)} %param.17, bf16[32,4096]{1,0:T(8,128)(2,1)S(1)} %all_gather.39, bf16[4096,896]{1,0:T(8,128)(2,1)} %param.16, bf16[32,3584]{1,0:T(8,128)(2,1)S(1)} %copy-done.5, s32[]{:T(128)S(6)} %select_n.38), kind=kOutput, calls=%fused_computation.15 | convolution fusion | flops 440602624 | bytes 14311428 | tf_op jit(solution)/shard_map/dot_general | solution.py:114
  107.7 20.4 %all-gather = bf16[128,3584]{1,0:T(8,128)(2,1)S(1)} all-gather(bf16[32,3584]{1,0:T(8,128)(2,1)} %convolution_convert_fusion.1), channel_id=2, replica_groups=mesh['seq'=8,'head'=4] {'head'}, dimensions={0}, use_global_device_ids=true | all-gather | bytes 1146880 | tf_op jit(solution)/shard_map/all_gather | solution.py:115
  128.5 4.6 %convolution_convert_fusion.8 = bf16[32,1024]{1,0:T(8,128)(2,1)S(1)} fusion(bf16[3584,1024]{1,0:T(8,128)(2,1)} %param.13, bf16[32,3584]{1,0:T(8,128)(2,1)S(1)} %reduce_sum.158, f32[32]{0:T(128)S(1)} %add_rsqrt_fusion.2, f32[3584]{0:T(1024)S(1)} %convert_element_type.163), kind=kOutput, calls=%fused_computation.85 | convolution fusion | flops 235372544 | bytes 7649408 | tf_op jit(solution)/shard_map/dot_general | solution.py:74
  136.1 3.2 %fusion = (f32[2,2,256]{2,1,0:T(2,128)S(1)}, f32[2,2048,256,2]{2,1,3,0:T(8,128)S(1)}) fusion(pred[256,2048]{0,1:T(8,128)(4,1)S(1)} %copy-done.7, bf16[256,2,2,256]{3,2,1,0:T(2,128)(2,1)S(1)} %copy-done.10, bf16[2048,2,256,1]{2,1,0,3:T(2,128)(2,1)} %bitcast.247), kind=kOutput, calls=%fused_computation.4 | convolution fusion | flops 1080032256 | bytes 11538432 | tf_op jit(solution)/shard_map/rhgd,khd->hgrk/dot_general | solution.py:31
  148.5 4.0 %reshape.319 = bf16[2048,2,256]{2,1,0:T(2,128)(2,1)} reshape(bf16[2048,512]{1,0:T(8,128)(2,1)} %all-gather.17.cloned.1.call-done) | data formatting | bytes 4194304 | tf_op jit(solution)/shard_map/reshape | solution.py:29
  152.5 4.8 %copy.83 = bf16[2048,2,256,1]{0,2,3,1:T(8,128)(2,1)S(1)} copy(bf16[2048,2,256,1]{2,1,0,3:T(2,128)(2,1)} %bitcast.251) | data formatting | bytes 4194304 | tf_op jit(solution)/shard_map/reshape | solution.py:29
  157.4 4.0 %reshape.318 = bf16[2048,2,256]{2,1,0:T(2,128)(2,1)} reshape(bf16[2048,512]{1,0:T(8,128)(2,1)} %all-gather.15.cloned.1.call-done) | data formatting | bytes 4194304 | tf_op jit(solution)/shard_map/reshape | solution.py:28
  161.7 3.2 %fusion.1 = (f32[2,2,256]{2,1,0:T(2,128)S(1)}, f32[2,2048,256,2]{2,1,3,0:T(8,128)S(1)}) fusion(pred[256,2048]{0,1:T(8,128)(4,1)S(1)} %copy-done.6, bf16[256,2,2,256]{3,2,1,0:T(2,128)(2,1)S(1)} %copy-done.8, bf16[2048,2,256,1]{2,1,0,3:T(2,128)(2,1)} %bitcast.248), kind=kOutput, calls=%fused_computation.5 | convolution fusion | flops 1080032256 | bytes 11538432 | tf_op jit(solution)/shard_map/rhgd,khd->hgrk/dot_general | solution.py:31
  174.5 16.2 %all_gather.45 = bf16[32,4096]{1,0:T(8,128)(2,1)S(1)} all-gather(bf16[32,1024]{1,0:T(8,128)(2,1)S(1)} %convert_element_type.208), channel_id=1, replica_groups=mesh['seq'=8,'head'=4] {'head'}, dimensions={1}, use_global_device_ids=true | all-gather | bytes 327680 | tf_op jit(solution)/shard_map/all_gather | solution.py:106
  190.7 7.3 %convolution_convert_fusion = bf16[32,3584]{1,0:T(8,128)(2,1)S(1)} fusion(bf16[896,3584]{1,0:T(8,128)(2,1)} %param.17, bf16[32,4096]{1,0:T(8,128)(2,1)S(1)} %all_gather.45, bf16[4096,896]{1,0:T(8,128)(2,1)} %param.16, bf16[32,3584]{1,0:T(8,128)(2,1)S(1)} %reduce_sum.158, s32[]{:T(128)S(6)} %select_n.38), kind=kOutput, calls=%fused_computation.14 | convolution fusion | flops 440602624 | bytes 14311428 | tf_op jit(solution)/shard_map/dot_general | solution.py:114
  198.0 23.0 %all-gather.1 = bf16[128,3584]{1,0:T(8,128)(2,1)S(1)} all-gather(bf16[32,3584]{1,0:T(8,128)(2,1)S(1)} %convolution_convert_fusion), channel_id=3, replica_groups=mesh['seq'=8,'head'=4] {'head'}, dimensions={0}, use_global_device_ids=true | all-gather | bytes 1146880 | tf_op jit(solution)/shard_map/all_gather | solution.py:115
  221.8 6.2 %fusion.51 = bf16[1,256,896]{2,1,0:T(8,128)(2,1)S(1)} fusion(bf16[256,4096]{0,1:T(8,128)(2,1)} %all-gather.13.cloned.1.call-done, bf16[4096,896]{1,0:T(8,128)(2,1)} %param.16, bf16[1,256,3584]{2,1,0:T(8,128)(2,1)} %get-tuple-element.16, s32[]{:T(128)S(6)} %select_n.38), kind=kOutput, calls=%fused_computation.60 | convolution fusion | flops 1879736320 | bytes 10354692 | tf_op jit(solution)/shard_map/dot_general | solution.py:100
  228.1 19.7 %all-gather.19.cloned.1.call-done = bf16[256,4096]{0,1:T(8,128)(2,1)} async-done(((bf16[256,1024]{0,1:T(8,128)(2,1)}), bf16[256,4096]{0,1:T(8,128)(2,1)}) %all-gather.19.cloned.1.call-update) | async-done | bytes 2097168 | tf_op jit(solution)/shard_map/all_gather | solution.py:101
  247.8 6.2 %fusion.50 = bf16[1,256,896]{2,1,0:T(8,128)(2,1)S(1)} fusion(bf16[256,4096]{0,1:T(8,128)(2,1)} %all-gather.19.cloned.1.call-done, bf16[4096,896]{1,0:T(8,128)(2,1)} %param.16, bf16[1,256,3584]{2,1,0:T(8,128)(2,1)} %get-tuple-element.17, s32[]{:T(128)S(6)} %select_n.38), kind=kOutput, calls=%fused_computation.59 | convolution fusion | flops 1879736320 | bytes 10354692 | tf_op jit(solution)/shard_map/dot_general | solution.py:100
  (139 shorter events, 47.0 us)
Async XLA Ops:
  7.2 43.0 %all-gather.9.cloned.1.call-start = ((), (), s32[]{:S(2)}) async-start(), calls=%async_computation | async-start | bytes 2359296 | tf_op jit(solution)/shard_map/all_gather | solution.py:87
  15.1 60.4 %all-gather.11.cloned.1.call-start = ((), (), s32[]{:S(2)}) async-start(), calls=%async_computation.1 | async-start | bytes 2359296 | tf_op jit(solution)/shard_map/all_gather | solution.py:88
  19.6 128.9 %all-gather.17.cloned.1.call-start = ((), (), s32[]{:S(2)}) async-start(), calls=%async_computation.4 | async-start | bytes 2359296 | tf_op jit(solution)/shard_map/all_gather | solution.py:88
  24.2 5.0 %copy-start.5 = (bf16[32,3584]{1,0:T(8,128)(2,1)S(1)}, bf16[32,3584]{1,0:T(8,128)(2,1)}, u32[]{:S(2)}) copy-start(bf16[32,3584]{1,0:T(8,128)(2,1)} %param.11) | copy-start | bytes 688132
  24.2 133.2 %all-gather.15.cloned.1.call-start = ((), (), s32[]{:S(2)}) async-start(), calls=%async_computation.3 | async-start | bytes 2359296 | tf_op jit(solution)/shard_map/all_gather | solution.py:87
  29.0 192.9 %all-gather.13.cloned.1.call-start = ((), (), s32[]{:S(2)}) async-start(), calls=%async_computation.2 | async-start | bytes 2621440 | tf_op jit(solution)/shard_map/all_gather | solution.py:101
  29.4 8.6 %slice-start = ((s8[7340032]{0:T(1024)(128)(4,1)}), s8[4194304]{0:T(1024)(128)(4,1)S(1)}, s32[]{:S(2)}) async-start(s8[7340032]{0:T(1024)(128)(4,1)} %bitcast.244), calls=%async_computation.6 | async-start | bytes 8388608
  32.4 5.6 %slice-start.1 = ((s8[7340032]{0:T(1024)(128)(4,1)}), s8[3145728]{0:T(1024)(128)(4,1)S(1)}, s32[]{:S(2)}) async-start(s8[7340032]{0:T(1024)(128)(4,1)} %bitcast.244), calls=%async_computation.7 | async-start | bytes 6291456
  33.2 5.0 %copy-start.1 = (bf16[2,256,3584]{2,1,0:T(8,128)(2,1)S(1)}, bf16[2,256,3584]{2,1,0:T(8,128)(2,1)}, u32[]{:S(2)}) copy-start(bf16[2,256,3584]{2,1,0:T(8,128)(2,1)} %param.9) | copy-start | bytes 11010052
  44.6 39.9 %copy-start.13 = (bf16[32,2,256]{2,1,0:T(2,128)(2,1)}, bf16[32,2,256]{2,1,0:T(2,128)(2,1)S(1)}, u32[]{:S(2)}) copy-start(bf16[32,2,256]{2,1,0:T(2,128)(2,1)S(1)} %reshape.311) | copy-start | bytes 98308
  45.0 7.7 %copy-start.9 = (bf16[256,2,2,256]{3,2,1,0:T(2,128)(2,1)}, bf16[256,2,2,256]{3,2,1,0:T(2,128)(2,1)S(1)}, u32[]{:S(2)}) copy-start(bf16[256,2,2,256]{3,2,1,0:T(2,128)(2,1)S(1)} %reshape.310) | copy-start | bytes 1572868
  45.2 4.9 %copy-start.20 = (f32[2,2,32]{2,1,0:T(2,128)}, f32[2,2,32]{2,1,0:T(2,128)S(1)}, u32[]{:S(2)}) copy-start(f32[2,2,32]{2,1,0:T(2,128)S(1)} %get-tuple-element.26) | copy-start | bytes 1540
  45.5 4.7 %copy-start.11 = (f32[2,2,256,32]{2,3,1,0:T(8,128)}, f32[2,2,256,32]{2,3,1,0:T(8,128)S(1)}, u32[]{:S(2)}) copy-start(f32[2,2,256,32]{2,3,1,0:T(8,128)S(1)} %get-tuple-element.33) | copy-start | bytes 393220
  45.5 4.6 %copy-start.16 = (f32[2,2,256]{2,1,0:T(2,128)}, f32[2,2,256]{2,1,0:T(2,128)S(1)}, u32[]{:S(2)}) copy-start(f32[2,2,256]{2,1,0:T(2,128)S(1)} %get-tuple-element.32) | copy-start | bytes 12292
  52.8 26.6 %copy-start.4 = (bf16[2048,2,256]{2,1,0:T(2,128)(2,1)}, bf16[2048,2,256]{2,1,0:T(2,128)(2,1)S(1)}, u32[]{:S(2)}) copy-start(bf16[2048,2,256]{2,1,0:T(2,128)(2,1)S(1)} %reshape.312) | copy-start | bytes 6291460
  54.2 29.9 %copy-start.22 = (f32[2,2,32]{2,1,0:T(2,128)S(1)}, f32[2,2,32]{2,1,0:T(2,128)}, u32[]{:S(2)}) copy-start(f32[2,2,32]{2,1,0:T(2,128)} %get-tuple-element.24) | copy-start | bytes 1540
  79.4 5.1 %copy-start.21 = (f32[2,2,32]{2,1,0:T(2,128)S(1)}, f32[2,2,32]{2,1,0:T(2,128)}, u32[]{:S(2)}) copy-start(f32[2,2,32]{2,1,0:T(2,128)} %copy-done.20) | copy-start | bytes 1540
  79.4 5.1 %copy-start.26 = (f32[2,2,32]{2,1,0:T(2,128)S(1)}, f32[2,2,32]{2,1,0:T(2,128)}, u32[]{:S(2)}) copy-start(f32[2,2,32]{2,1,0:T(2,128)} %fusion.96) | copy-start | bytes 1540
  128.4 4.6 %copy-start.27 = (f32[32]{0:T(128)}, f32[32]{0:T(128)S(1)}, u32[]{:S(2)}) copy-start(f32[32]{0:T(128)S(1)} %add_rsqrt_fusion.2) | copy-start | bytes 388
  141.6 5.7 %copy-start.18 = (f32[2,2,32]{2,1,0:T(2,128)}, f32[2,2,32]{2,1,0:T(2,128)S(1)}, u32[]{:S(2)}) copy-start(f32[2,2,32]{2,1,0:T(2,128)S(1)} %get-tuple-element.36) | copy-start | bytes 1540
  147.0 100.8 %all-gather.19.cloned.1.call-start = ((), (), s32[]{:S(2)}) async-start(), calls=%async_computation.5 | async-start | bytes 2621440 | tf_op jit(solution)/shard_map/all_gather | solution.py:101
  152.5 8.8 %copy-start.8 = (bf16[256,2,2,256]{3,2,1,0:T(2,128)(2,1)S(1)}, bf16[256,2,2,256]{3,2,1,0:T(2,128)(2,1)}, u32[]{:S(2)}) copy-start(bf16[256,2,2,256]{3,2,1,0:T(2,128)(2,1)} %reshape.316) | copy-start | bytes 1572868
  152.5 9.2 %copy-start.6 = (pred[256,2048]{0,1:T(8,128)(4,1)S(1)}, pred[256,2048]{0,1:T(8,128)(4,1)}, u32[]{:S(2)}) copy-start(pred[256,2048]{0,1:T(8,128)(4,1)} %get-tuple-element.21) | copy-start | bytes 1572868
  169.4 4.0 %copy-start.19 = (f32[2,2,32]{2,1,0:T(2,128)S(1)}, f32[2,2,32]{2,1,0:T(2,128)}, u32[]{:S(2)}) copy-start(f32[2,2,32]{2,1,0:T(2,128)} %copy-done.18) | copy-start | bytes 1540
  (13 other events, 35.0 us)
Sparse Core Ops, SparseCore 0:
  15.2 30.4 all-gather.8
  47.6 27.7 all-gather.10
  77.3 27.7 all-gather.16
  106.9 27.7 all-gather.14
  147.1 49.6 all-gather.12
  198.7 48.9 all-gather.18
